TPU v7x, 32 devices: a whole 2x2x4 slice. The times are simulated.
32 devices in a mesh: samp: 8 (over y, x, core), snp: 4 (over z).
Axes of the slice: x: 2, y: 2, z: 4, core: 2. Of those that a mesh axis runs over, the one named last changes fastest.
Arguments:
- genotypes: bfloat16 [8192, 16384], P('samp', 'snp'), may hold values from -6 to 6
- probes: bfloat16 [8, 8192], P(None, 'samp'), may hold values from -6 to 6
- env_label: int32 [8192], P('samp'), may hold values from 0 to 7
- variances: float32 [3], replicated, may hold values from 0.25 to 1
Outputs:
- first: float32 [8, 8192], P(None, 'samp')
- second: float32 [8, 8192], P(None, 'samp')
All inputs are finite; a program needn't handle non-finite values.
Results may differ from a plain program's by a relative error of at most 0.0018.
Values may be sent and summed in bfloat16 or wider, within the bound.
A program may use at most 64 MiB of HBM per device.

v0:
```python
import jax
import jax.numpy as jnp
from jax import lax
from jax.sharding import PartitionSpec as P

SNPS = 16384
PROBES = 8
ENVS = 8


def local_image(snp_panel, genotypes):
    return lax.dot_general(
        snp_panel, genotypes, (((1,), (1,)), ((), ())), preferred_element_type=jnp.float32
    )


def apply_operator(current, genotypes, onehot, variances):
    rounded = current.astype(jnp.bfloat16)
    scaled = (onehot[:, None, :] * rounded[None, :, :]).reshape(ENVS * PROBES, -1)
    panel = jnp.concatenate([rounded, scaled], axis=0)
    partial_panel = jnp.dot(panel, genotypes, preferred_element_type=jnp.float32)
    snp_panel = lax.psum(partial_panel, "samp").astype(jnp.bfloat16)
    image = local_image(snp_panel, genotypes)
    additive = image[:PROBES]
    blocks = image[PROBES:].reshape(ENVS, PROBES, -1)
    interaction = jnp.sum(onehot.astype(jnp.float32)[:, None, :] * blocks, axis=0)
    weighted = variances[0] * additive / SNPS + variances[1] * interaction / SNPS
    totals = lax.psum(weighted, "snp")
    return totals + variances[2] * current


def per_device(genotypes, probes, env_label, variances):
    labels = jnp.arange(ENVS, dtype=jnp.int32)
    onehot = (env_label[None, :] == labels[:, None]).astype(jnp.bfloat16)
    first = apply_operator(probes.astype(jnp.float32), genotypes, onehot, variances)
    second = apply_operator(first, genotypes, onehot, variances)
    return (first, second)


def solution(mesh):
    return jax.shard_map(
        per_device,
        mesh=mesh,
        in_specs=(P("samp", "snp"), P(None, "samp"), P("samp"), P()),
        out_specs=(P(None, "samp"), P(None, "samp")),
        check_vma=False,
    )
```

profile of v0, /device:TPU:0, one launch (start us, length us, event | category | flops | bytes accessed | tf_op | source)
XLA Modules:
  0.0 167.7 jit_solution(6879203342592267592)
XLA Ops:
  0.6 1.4 fusion.25
  2.1 0.7 fusion.21
  2.8 0.7 multiply_bitcast_fusion.1
  3.5 5.0 %fusion.8 = f32[72,4096]{1,0:T(8,128)S(1)} fusion(bf16[1024,4096]{1,0:T(8,128)(2,1)} %param.4, bf16[64,1024]{1,0:T(8,128)(2,1)S(1)} %multiply_bitcast_fusion.1, bf16[8,1024]{1,0:T(8,128)(2,1)} %param.5), kind=kOutput, calls=%fused_computation.10 | convolution fusion | flops 604274688 | bytes 9715712 | tf_op jit(solution)/shard_map/dot_general | solution.py:21
  8.5 0.0 copy-start
  8.5 53.0 %all-reduce.2 = bf16[72,4096]{1,0:T(8,128)(2,1)S(1)} all-reduce(f32[72,4096]{1,0:T(8,128)S(1)} %fusion.8), channel_id=1, replica_groups=mesh['samp'=8,'snp'=4] {'samp'}, use_global_device_ids=true, to_apply=%region_0.0 | all-reduce | flops 294912 | bytes 1769472 | tf_op jit(solution)/shard_map/psum | solution.py:22
  61.5 6.0 %fusion.27 = f32[72,1024]{1,0:T(8,128)S(1)} fusion(bf16[72,4096]{1,0:T(8,128)(2,1)S(1)} %all-reduce.2, bf16[1024,4096]{1,0:T(8,128)(2,1)} %param.4), kind=kOutput, calls=%fused_computation.36 | convolution fusion | flops 603979776 | bytes 9273344 | tf_op jit(solution)/shard_map/dot_general | solution.py:12
  67.6 1.2 fusion.19
  68.8 19.5 %psum.29 = f32[8,1024]{1,0:T(8,128)S(1)} all-reduce(f32[8,1024]{1,0:T(8,128)S(1)} %fusion.19), channel_id=1, replica_groups=mesh['samp'=8,'snp'=4] {'snp'}, use_global_device_ids=true, to_apply=%region_2.0 | all-reduce | flops 8192 | bytes 65536 | tf_op jit(solution)/shard_map/psum | solution.py:28
  88.3 0.0 copy-done
  88.3 0.7 fusion.24
  89.0 0.0 copy-start.1
  89.1 5.0 %fusion.12 = f32[72,4096]{1,0:T(8,128)S(1)} fusion(bf16[1024,4096]{1,0:T(8,128)(2,1)} %param.4, bf16[64,1024]{1,0:T(8,128)(2,1)S(1)} %multiply_bitcast_fusion, bf16[8,1024]{1,0:T(8,128)(2,1)S(1)} %get-tuple-element.2), kind=kOutput, calls=%fused_computation.14 | convolution fusion | flops 604274688 | bytes 9715712 | tf_op jit(solution)/shard_map/dot_general | solution.py:21
  94.1 49.2 %all-reduce.3 = bf16[72,4096]{1,0:T(8,128)(2,1)S(1)} all-reduce(f32[72,4096]{1,0:T(8,128)S(1)} %fusion.12), channel_id=1, replica_groups=mesh['samp'=8,'snp'=4] {'samp'}, use_global_device_ids=true, to_apply=%region_3.0 | all-reduce | flops 294912 | bytes 1769472 | tf_op jit(solution)/shard_map/psum | solution.py:22
  143.3 6.0 %fusion.26 = f32[72,1024]{1,0:T(8,128)S(1)} fusion(bf16[72,4096]{1,0:T(8,128)(2,1)S(1)} %all-reduce.3, bf16[1024,4096]{1,0:T(8,128)(2,1)} %param.4), kind=kOutput, calls=%fused_computation.35 | convolution fusion | flops 603979776 | bytes 9273344 | tf_op jit(solution)/shard_map/dot_general | solution.py:12
  149.4 1.2 fusion.17
  150.6 15.8 %psum.31 = f32[8,1024]{1,0:T(8,128)S(1)} all-reduce(f32[8,1024]{1,0:T(8,128)S(1)} %fusion.17), channel_id=1, replica_groups=mesh['samp'=8,'snp'=4] {'snp'}, use_global_device_ids=true, to_apply=%region_5.0 | all-reduce | flops 8192 | bytes 65536 | tf_op jit(solution)/shard_map/psum | solution.py:28
  166.4 0.0 copy-done.1
  166.4 1.3 multiply_add_fusion
  (3 shorter events, 0.1 us)
Async XLA Ops:
  8.5 79.8 %copy-start = (bf16[8,1024]{1,0:T(8,128)(2,1)S(1)}, bf16[8,1024]{1,0:T(8,128)(2,1)}, u32[]{:S(2)}) copy-start(bf16[8,1024]{1,0:T(8,128)(2,1)} %param.5) | copy-start | bytes 49156
  89.0 77.4 %copy-start.1 = (f32[8,1024]{1,0:T(8,128)}, f32[8,1024]{1,0:T(8,128)S(1)}, u32[]{:S(2)}) copy-start(f32[8,1024]{1,0:T(8,128)S(1)} %get-tuple-element.3) | copy-start | bytes 98308
where the time goes:
time: 168 us
  blocking collectives  138 us (82%)
  matrix products  22.1 us (13%)
  other arithmetic  5.97 us (4%)
    psum x2, blocking collectives, apply_operator(): snp_panel = lax.psum(partial_panel, 'samp').astype(jnp.bfloat16)  102 us
    psum x2, blocking collectives, apply_operator(): totals = lax.psum(weighted, 'snp')  35.2 us
    dot_general x2, matrix products, local_image(): lax.dot_general(snp_panel, genotypes, (((1,), (1,)), ((), ())), preferred...  12.1 us
    dot_general x2, matrix products, apply_operator(): jnp.dot(panel, genotypes, preferred_element_type=jnp.float32)  9.96 us

commit v1 on v0

v1 whole, which is shorter than its diff:
```python
import functools

import jax
import jax.numpy as jnp
from jax import lax
from jax.experimental import pallas as pl
from jax.experimental.pallas import tpu as pltpu
from jax.sharding import PartitionSpec as P

ENVS = 8


def plan(samp, cols):
    chips = samp // 2
    share = cols // samp
    stages = 2 if share % 256 == 0 else 1
    return chips, share, stages, share // stages


def kernel(
    samp, snp, z_hbm, probes_ref, label_ref, var_ref, first_ref, second_ref,
    z, panel, onehot, mine, pair_out, pair_in, rs_out, rs_in, ag, image, weighted, z_in,
    load_sem, pair_s, pair_r, rs_s, rs_r, ag_s, ag_r, fw_s, fw_r, zs_s, zs_r,
):
    probes, local = probes_ref.shape
    cols = z.shape[1]
    rows = ENVS * probes
    chips, share, stages, sub = plan(samp, cols)
    me = lax.axis_index("samp")
    chip, core = me // 2, me % 2
    here = lax.axis_index("snp")

    def device(other_chip, other_core):
        return {"samp": other_chip * 2 + other_core}

    def ahead(r):
        return lax.rem(chip + r, chips)

    def behind(r):
        return lax.rem(chip - r + chips, chips)

    def start_of(which_core, which_chip, j):
        return pl.multiple_of((which_core * chips + which_chip) * share + j * sub, 128)

    def load(j, away, k):
        side = (1 - core) if away else core
        at = pl.ds(start_of(side, k, j), sub)
        return pltpu.make_async_copy(z_hbm.at[:, at], z.at[:, at], load_sem.at[j, int(away), k])

    for j in range(stages):
        for away in (True, False):
            for k in range(chips):
                load(j, away, k).start()

    barrier = pltpu.get_barrier_semaphore()
    peers = [device(chip, 1 - core)]
    peers += [device(ahead(r), core) for r in range(1, chips)]
    peers += [{"snp": lax.rem(here + r, snp)} for r in range(1, snp)]
    for peer in peers:
        pl.semaphore_signal(barrier, inc=1, device_id=peer, device_id_type=pl.DeviceIdType.MESH)

    labels = label_ref[...]
    for e in range(ENVS):
        onehot[e * probes:(e + 1) * probes, :] = jnp.broadcast_to(
            (labels == e).astype(jnp.float32), (probes, local))

    def remote(src, dst, send, recv, to):
        return pltpu.make_async_remote_copy(
            src_ref=src, dst_ref=dst, send_sem=send, recv_sem=recv,
            device_id=to, device_id_type=pl.DeviceIdType.MESH)

    sent = []
    for op in range(2):
        current = probes_ref[...].astype(jnp.float32) if op == 0 else first_ref[...]
        rounded = current.astype(jnp.bfloat16).astype(jnp.float32)
        for e in range(ENVS):
            block = slice(e * probes, (e + 1) * probes)
            panel[block, :] = (onehot[block, :] * rounded).astype(jnp.bfloat16)

        def matmul(away, j, k):
            side = (1 - core) if away else core
            if op == 0:
                load(j, away, k).wait()
            return jnp.dot(panel[...], z[:, pl.ds(start_of(side, k, j), sub)], preferred_element_type=jnp.float32)

        def pair(j):
            return remote(pair_out.at[op, j], pair_in.at[op, j], pair_s.at[op, j], pair_r.at[op, j],
                          device(chip, 1 - core))

        def scatter(j, r):
            return remote(rs_out.at[op, j, r], rs_in.at[op, j, r], rs_s.at[op, j, r], rs_r.at[op, j, r],
                          device(ahead(r), core))

        def gather(j, r):
            at = ag.at[op, j, core, chip]
            return remote(at, at, ag_s.at[op, j, r], ag_r.at[op, j, r], device(ahead(r), core))

        def forward(j, r):
            at = ag.at[op, j, core, behind(r)]
            return remote(at, at, fw_s.at[op, j, r], fw_r.at[op, j, r], device(chip, 1 - core))

        def send(copy):
            copy.start()
            sent.append(copy)

        def away_part(j):
            def body(k, _):
                pair_out[op, j, k] = matmul(True, j, k)
                return 0
            lax.fori_loop(0, chips, body, 0)
            if op == 0 and j == 0:
                pl.semaphore_wait(barrier, len(peers))
            send(pair(j))

        def own_part(j):
            def body(k, _):
                mine[j, k] = matmul(False, j, k)
                return 0
            lax.fori_loop(0, chips, body, 0)

        def reduce_pair(j):
            pair(j).wait_recv()
            for r in range(1, chips):
                k = ahead(r)
                rs_out[op, j, r] = mine[j, k] + pair_in[op, j, k]
                send(scatter(j, r))

        def finish_panel(j):
            total = mine[j, chip] + pair_in[op, j, chip]
            for r in range(1, chips):
                scatter(j, r).wait_recv()
                total = total + rs_in[op, j, r]
            plain = total[:probes]
            for e in range(1, ENVS):
                plain = plain + total[e * probes:(e + 1) * probes]
            ag[op, j, core, chip] = jnp.concatenate([plain, total], axis=0).astype(jnp.bfloat16)
            for r in range(1, chips):
                send(gather(j, r))
            send(forward(j, 0))

        def add_image(j, which_core, which_chip):
            part = lax.dot_general(
                ag[op, j, which_core, which_chip], z[:, pl.ds(start_of(which_core, which_chip, j), sub)],
                (((1,), (1,)), ((), ())), preferred_element_type=jnp.float32)
            image[...] += part

        away_part(0)
        own_part(0)
        for j in range(1, stages):
            away_part(j)
            reduce_pair(j - 1)
            own_part(j)
        reduce_pair(stages - 1)
        image[...] = jnp.zeros_like(image)
        for j in range(stages):
            finish_panel(j)
        for j in range(stages):
            add_image(j, core, chip)
        for j in range(stages):
            for r in range(1, chips):
                gather(j, r).wait_recv()
                send(forward(j, r))
                add_image(j, core, behind(r))
            for r in range(chips):
                forward(j, r).wait_recv()
                add_image(j, 1 - core, behind(r))

        total_snps = cols * snp
        interaction = jnp.zeros((probes, local), jnp.float32)
        for e in range(ENVS):
            block = slice(e * probes, (e + 1) * probes)
            interaction = interaction + onehot[block, :] * image[probes + e * probes:probes + (e + 1) * probes, :]
        weighted[op] = var_ref[0] * image[:probes, :] / total_snps + var_ref[1] * interaction / total_snps

        def over_snps(r):
            return remote(weighted.at[op], z_in.at[op, r], zs_s.at[op, r], zs_r.at[op, r],
                          {"snp": lax.rem(here + r, snp)})

        for r in range(1, snp):
            send(over_snps(r))
        for r in range(1, snp):
            over_snps(r).wait_recv()
        parts = [weighted[op]] + [z_in[op, r] for r in range(1, snp)]
        total = jnp.zeros((probes, local), jnp.float32)
        for s in range(snp):
            term = parts[0]
            for r in range(1, snp):
                term = jnp.where(lax.rem(here - r + snp, snp) == s, parts[r], term)
            total = total + term
        out = first_ref if op == 0 else second_ref
        out[...] = total + var_ref[2] * current
    for copy in sent:
        copy.wait_send()


def solution(mesh):
    samp, snp = mesh.shape["samp"], mesh.shape["snp"]

    def per_device(genotypes, probes, env_label, variances):
        local, cols = genotypes.shape
        count = probes.shape[0]
        rows = ENVS * count
        chips, _, stages, sub = plan(samp, cols)
        vmem = pltpu.VMEM
        dma = pltpu.SemaphoreType.DMA
        out = jax.ShapeDtypeStruct((count, local), jnp.float32)
        whole = pl.BlockSpec(memory_space=pltpu.VMEM)
        return pl.pallas_call(
            functools.partial(kernel, samp, snp),
            out_shape=(out, out),
            in_specs=[pl.BlockSpec(memory_space=pl.ANY), whole, whole, pl.BlockSpec(memory_space=pltpu.SMEM)],
            out_specs=(whole, whole),
            scratch_shapes=[
                vmem((local, cols), jnp.bfloat16),
                vmem((rows, local), jnp.bfloat16),
                vmem((rows, local), jnp.float32),
                vmem((stages, chips, rows, sub), jnp.float32),
                vmem((2, stages, chips, rows, sub), jnp.float32),
                vmem((2, stages, chips, rows, sub), jnp.float32),
                vmem((2, stages, chips, rows, sub), jnp.float32),
                vmem((2, stages, chips, rows, sub), jnp.float32),
                vmem((2, stages, 2, chips, rows + count, sub), jnp.bfloat16),
                vmem((rows + count, local), jnp.float32),
                vmem((2, count, local), jnp.float32),
                vmem((2, snp, count, local), jnp.float32),
                dma((stages, 2, chips)),
                dma((2, stages)), dma((2, stages)),
                dma((2, stages, chips)), dma((2, stages, chips)),
                dma((2, stages, chips)), dma((2, stages, chips)),
                dma((2, stages, chips)), dma((2, stages, chips)),
                dma((2, snp)), dma((2, snp)),
            ],
            compiler_params=pltpu.CompilerParams(
                collective_id=0, has_side_effects=True, vmem_limit_bytes=56 * 1024 * 1024),
        )(genotypes, probes, env_label.reshape(1, local), variances)

    return jax.shard_map(
        per_device,
        mesh=mesh,
        in_specs=(P("samp", "snp"), P(None, "samp"), P("samp"), P()),
        out_specs=(P(None, "samp"), P(None, "samp")),
        check_vma=False,
    )
```

time: 168 us -> 52.6 us (0.31)
  blocking collectives: 138 us -> 0 us
  Pallas kernels: 0 us -> 48.9 us
  matrix products: 22.1 us -> 0 us
  other arithmetic: 5.97 us -> 0 us
    psum x4 -> x0, blocking collectives: 138 us -> none  [the longest x2 102 us: apply_operator(): snp_panel = lax.psum(partial_panel, 'samp').astype(jnp.bfloat16)]
    pallas_call x0 -> x1, Pallas kernels: none -> 48.9 us  [per_device(): pl.pallas_call(functools.partial(kernel, samp, snp), out_shape=(out, out)...]
    dot_general x4 -> x0, matrix products: 22.1 us -> none  [the longest x2 12.1 us: local_image(): lax.dot_general(snp_panel, genotypes, (((1,), (1,)), ((), ())), preferred...]
    add x3 -> x0, other arithmetic: 3.74 us -> none  [the longest x2 2.43 us: apply_operator(): variances[0] * additive / SNPS + variances[1] * interaction / SNPS]
    unnamed x4 -> x2, local copies, waits for them, and re-layouts: 0.01 us -> 2.75 us
where the time goes in v1:
time: 52.6 us; the launch traced here: 52.3 us
  Pallas kernels  48.9 us (93%)
  local copies, waits for them, and re-layouts  2.75 us (5%)
  between operations  0.64 us (1%)
    pallas_call x1, Pallas kernels, per_device(): pl.pallas_call(functools.partial(kernel, samp, snp), out_shape=(out, out)...  48.9 us
    unnamed x2, local copies, waits for them, and re-layouts  2.75 us

profile of v1, /device:TPU:0, one launch (start us, length us, event | category | flops | bytes accessed | tf_op | source)
XLA Modules:
  0.0 52.3 jit_solution(3376336345794204198)
XLA Ops:
  0.6 48.9 %shard_map.59 = (f32[8,1024]{1,0:T(8,128)}, f32[8,1024]{1,0:T(8,128)}) custom-call(bf16[1024,4096]{1,0:T(8,128)(2,1)} %z_hbm.1, bf16[8,1024]{1,0:T(8,128)(2,1)} %probes_ref.1, s32[1,1024]{1,0:T(1,128)} %bitcast.1, f32[3]{0:T(128)} %var_ref.1), custom_call_target="tpu_custom_call" | custom-call | tf_op jit(solution)/shard_map/pallas_call | solution.py:208
  49.5 1.4 %copy.8 = f32[8,1024]{1,0:T(8,128)} copy(f32[8,1024]{1,0:T(8,128)} %get-tuple-element.4) | data formatting | bytes 65536
  50.9 1.4 %copy.9 = f32[8,1024]{1,0:T(8,128)} copy(f32[8,1024]{1,0:T(8,128)} %get-tuple-element.5) | data formatting | bytes 65536

commit v2 on v1

v2 whole, which is shorter than its diff:
```python
import functools

import jax
import jax.numpy as jnp
from jax import lax
from jax.experimental import pallas as pl
from jax.experimental.pallas import tpu as pltpu
from jax.sharding import PartitionSpec as P

ENVS = 8


def plan(samp, cols):
    chips = samp // 2
    share = cols // samp
    stages = 2 if share % 256 == 0 else 1
    return chips, share, stages, share // stages


def kernel(
    samp, snp, z_hbm, probes_ref, label_ref, var_ref, first_ref, second_ref,
    z, panel, onehot, mine, pair_out, pair_in, rs_out, rs_in, ag, image, z_in,
    load_sem, pair_s, pair_r, rs_s, rs_r, ag_s, ag_r, fw_s, fw_r, zs_s, zs_r,
):
    probes, local = probes_ref.shape
    cols = z.shape[1]
    rows = ENVS * probes
    chips, share, stages, sub = plan(samp, cols)
    me = lax.axis_index("samp")
    chip, core = me // 2, me % 2
    here = lax.axis_index("snp")

    def device(other_chip, other_core):
        return {"samp": other_chip * 2 + other_core}

    def partner(r):
        if chips & (chips - 1):
            return lax.rem(chip + r, chips)
        return sum(lax.rem(chip // bit + r // bit, 2) * bit for bit in (1 << b for b in range(chips.bit_length() - 1)))

    def source(r):
        return lax.rem(chip - r + chips, chips) if chips & (chips - 1) else partner(r)

    width = chips * sub

    def start_of(which_core, j):
        return pl.multiple_of(which_core * (cols // 2) + j * width, 128)

    def columns(which_chip):
        return pl.ds(pl.multiple_of(which_chip * sub, 128), sub)

    def load(j, away):
        at = pl.ds(start_of((1 - core) if away else core, j), width)
        return pltpu.make_async_copy(z_hbm.at[:, at], z.at[:, at], load_sem.at[j, int(away)])

    for j in range(stages):
        for away in (True, False):
            load(j, away).start()

    barrier = pltpu.get_barrier_semaphore()
    peers = [device(chip, 1 - core)]
    peers += [device(partner(r), core) for r in range(1, chips)]
    peers += [{"snp": lax.rem(here + r, snp)} for r in range(1, snp)]
    for peer in peers:
        pl.semaphore_signal(barrier, inc=1, device_id=peer, device_id_type=pl.DeviceIdType.MESH)

    labels = label_ref[...]
    for e in range(ENVS):
        onehot[e * probes:(e + 1) * probes, :] = jnp.broadcast_to(
            (labels == e).astype(jnp.float32), (probes, local))

    def remote(src, dst, send, recv, to):
        return pltpu.make_async_remote_copy(
            src_ref=src, dst_ref=dst, send_sem=send, recv_sem=recv,
            device_id=to, device_id_type=pl.DeviceIdType.MESH)

    def sum_blocks(blocks):
        total = blocks[:probes]
        for e in range(1, ENVS):
            total = total + blocks[e * probes:(e + 1) * probes]
        return total

    sent = []
    for op in range(2):
        current = probes_ref[...].astype(jnp.float32) if op == 0 else first_ref[...]
        rounded = current.astype(jnp.bfloat16).astype(jnp.float32)
        for e in range(ENVS):
            block = slice(e * probes, (e + 1) * probes)
            panel[block, :] = (onehot[block, :] * rounded).astype(jnp.bfloat16)

        def matmul(away, j):
            if op == 0:
                load(j, away).wait()
            at = pl.ds(start_of((1 - core) if away else core, j), width)
            return jnp.dot(panel[...], z[:, at], preferred_element_type=jnp.float32)

        def pair(j):
            return remote(pair_out.at[op, j], pair_in.at[op, j], pair_s.at[op, j], pair_r.at[op, j],
                          device(chip, 1 - core))

        def scatter(j, r):
            return remote(rs_out.at[op, j, r], rs_in.at[op, j, r], rs_s.at[op, j, r], rs_r.at[op, j, r],
                          device(partner(r), core))

        def gather(j, r):
            at = ag.at[op, j, core, chip]
            return remote(at, at, ag_s.at[op, j, r], ag_r.at[op, j, r], device(partner(r), core))

        def forward(j, r):
            at = ag.at[op, j, core, source(r)]
            return remote(at, at, fw_s.at[op, j, r], fw_r.at[op, j, r], device(chip, 1 - core))

        def send(copy):
            copy.start()
            sent.append(copy)

        def away_part(j):
            pair_out[op, j] = matmul(True, j)

        def own_part(j):
            mine[j] = matmul(False, j)

        def reduce_pair(j):
            pair(j).wait_recv()
            for r in reversed(range(1, chips)):
                at = columns(partner(r))
                both = mine[j, :, at] + pair_in[op, j, :, at]
                short = both.astype(jnp.bfloat16)
                rest = both - short.astype(jnp.float32)
                lost = sum_blocks(rest).astype(jnp.bfloat16)
                rs_out[op, j, r] = jnp.concatenate([lost, short], axis=0)
                send(scatter(j, r))

        def finish_panel(j):
            at = columns(chip)
            total = mine[j, :, at] + pair_in[op, j, :, at]
            lost = jnp.zeros((probes, sub), jnp.float32)
            for r in range(1, chips):
                scatter(j, r).wait_recv()
                came = rs_in[op, j, r].astype(jnp.float32)
                total = total + came[probes:]
                lost = lost + came[:probes]
            plain = sum_blocks(total) + lost
            ag[op, j, core, chip] = jnp.concatenate([plain, total], axis=0).astype(jnp.bfloat16)
            for r in reversed(range(1, chips)):
                send(gather(j, r))
            send(forward(j, 0))

        def add_image(j, which_core, which_chip):
            at = pl.ds(pl.multiple_of(start_of(which_core, j) + which_chip * sub, 128), sub)
            part = lax.dot_general(
                ag[op, j, which_core, which_chip], z[:, at],
                (((1,), (1,)), ((), ())), preferred_element_type=jnp.float32)
            image[...] += part

        away_part(0)
        if op == 0:
            own_part(0)
            pl.semaphore_wait(barrier, len(peers))
        send(pair(0))
        if op == 1:
            own_part(0)
        for j in range(1, stages):
            away_part(j)
            send(pair(j))
            reduce_pair(j - 1)
            own_part(j)
        reduce_pair(stages - 1)
        image[...] = jnp.zeros_like(image)
        for j in range(stages):
            finish_panel(j)
        for j in range(stages):
            add_image(j, core, chip)
        for j in range(stages):
            for r in range(1, chips):
                gather(j, r).wait_recv()
                send(forward(j, r))
                add_image(j, core, source(r))
            for r in range(chips):
                forward(j, r).wait_recv()
                add_image(j, 1 - core, source(r))

        total_snps = cols * snp
        interaction = jnp.zeros((probes, local), jnp.float32)
        for e in range(ENVS):
            block = slice(e * probes, (e + 1) * probes)
            interaction = interaction + onehot[block, :] * image[probes + e * probes:probes + (e + 1) * probes, :]
        z_in[op, here] = var_ref[0] * image[:probes, :] / total_snps + var_ref[1] * interaction / total_snps

        def other_snp(r):
            return lax.rem(here + jnp.where(here < snp // 2, snp - r, r), snp)

        def over_snps(r, recv):
            return remote(z_in.at[op, here], z_in.at[op, here], zs_s.at[op, r], zs_r.at[op, recv],
                          {"snp": other_snp(r)})

        for r in range(1, snp):
            send(over_snps(r, here))
        for r in range(1, snp):
            over_snps(r, other_snp(r)).wait_recv()
        total = z_in[op, 0]
        for s in range(1, snp):
            total = total + z_in[op, s]
        out = first_ref if op == 0 else second_ref
        out[...] = total + var_ref[2] * current
    for copy in sent:
        copy.wait_send()


def solution(mesh):
    samp, snp = mesh.shape["samp"], mesh.shape["snp"]

    def per_device(genotypes, probes, env_label, variances):
        local, cols = genotypes.shape
        count = probes.shape[0]
        rows = ENVS * count
        chips, _, stages, sub = plan(samp, cols)
        vmem = pltpu.VMEM
        dma = pltpu.SemaphoreType.DMA
        out = jax.ShapeDtypeStruct((count, local), jnp.float32)
        whole = pl.BlockSpec(memory_space=pltpu.VMEM)
        return pl.pallas_call(
            functools.partial(kernel, samp, snp),
            out_shape=(out, out),
            in_specs=[pl.BlockSpec(memory_space=pl.ANY), whole, whole, pl.BlockSpec(memory_space=pltpu.SMEM)],
            out_specs=(whole, whole),
            scratch_shapes=[
                vmem((local, cols), jnp.bfloat16),
                vmem((rows, local), jnp.bfloat16),
                vmem((rows, local), jnp.float32),
                vmem((stages, rows, chips * sub), jnp.float32),
                vmem((2, stages, rows, chips * sub), jnp.float32),
                vmem((2, stages, rows, chips * sub), jnp.float32),
                vmem((2, stages, chips, rows + count, sub), jnp.bfloat16),
                vmem((2, stages, chips, rows + count, sub), jnp.bfloat16),
                vmem((2, stages, 2, chips, rows + count, sub), jnp.bfloat16),
                vmem((rows + count, local), jnp.float32),
                vmem((2, snp, count, local), jnp.float32),
                dma((stages, 2)),
                dma((2, stages)), dma((2, stages)),
                dma((2, stages, chips)), dma((2, stages, chips)),
                dma((2, stages, chips)), dma((2, stages, chips)),
                dma((2, stages, chips)), dma((2, stages, chips)),
                dma((2, snp)), dma((2, snp)),
            ],
            compiler_params=pltpu.CompilerParams(
                collective_id=0, has_side_effects=True, vmem_limit_bytes=56 * 1024 * 1024),
        )(genotypes, probes, env_label.reshape(1, local), variances)

    return jax.shard_map(
        per_device,
        mesh=mesh,
        in_specs=(P("samp", "snp"), P(None, "samp"), P("samp"), P()),
        out_specs=(P(None, "samp"), P(None, "samp")),
        check_vma=False,
    )
```

time: 52.6 us -> 46.2 us (0.88)
  Pallas kernels: 48.9 us -> 42.5 us
    pallas_call x1, Pallas kernels: 48.9 us -> 42.5 us  [per_device(): pl.pallas_call(functools.partial(kernel, samp, snp), out_shape=(out, out)...]
where the time goes in v2:
time: 46.2 us; the launch traced here: 45.9 us
  Pallas kernels  42.5 us (92%)
  local copies, waits for them, and re-layouts  2.75 us (6%)
  between operations  0.64 us (1%)
    pallas_call x1, Pallas kernels, per_device(): pl.pallas_call(functools.partial(kernel, samp, snp), out_shape=(out, out)...  42.5 us
    unnamed x2, local copies, waits for them, and re-layouts  2.75 us

profile of v2, /device:TPU:0, one launch (start us, length us, event | category | flops | bytes accessed | tf_op | source)
XLA Modules:
  0.0 45.9 jit_solution(8634618474583876576)
XLA Ops:
  0.6 42.5 %shard_map.59 = (f32[8,1024]{1,0:T(8,128)}, f32[8,1024]{1,0:T(8,128)}) custom-call(bf16[1024,4096]{1,0:T(8,128)(2,1)} %z_hbm.1, bf16[8,1024]{1,0:T(8,128)(2,1)} %probes_ref.1, s32[1,1024]{1,0:T(1,128)} %bitcast.1, f32[3]{0:T(128)} %var_ref.1), custom_call_target="tpu_custom_call" | custom-call | tf_op jit(solution)/shard_map/pallas_call | solution.py:222
  43.1 1.4 %copy.8 = f32[8,1024]{1,0:T(8,128)} copy(f32[8,1024]{1,0:T(8,128)} %get-tuple-element.4) | data formatting | bytes 65536
  44.5 1.4 %copy.9 = f32[8,1024]{1,0:T(8,128)} copy(f32[8,1024]{1,0:T(8,128)} %get-tuple-element.5) | data formatting | bytes 65536

commit v3 on v2

--- a/solution.py
+++ b/solution.py
@@ -18,11 +18,11 @@
 
 
 def kernel(
-    samp, snp, z_hbm, probes_ref, label_ref, var_ref, first_ref, second_ref,
-    z, panel, onehot, mine, pair_out, pair_in, rs_out, rs_in, ag, image, z_in,
-    load_sem, pair_s, pair_r, rs_s, rs_r, ag_s, ag_r, fw_s, fw_r, zs_s, zs_r,
+    samp, snp, z_hbm, probes_hbm, label_hbm, var_ref, first_ref, second_ref,
+    z, probes_ref, label_ref, panel, onehot, mine, pair_out, pair_in, rs_out, rs_in, ag, image, z_in,
+    load_sem, small_sem, pair_s, pair_r, rs_s, rs_r, ag_s, ag_r, fw_s, fw_r, zs_s, zs_r,
 ):
-    probes, local = probes_ref.shape
+    probes, local = probes_hbm.shape
     cols = z.shape[1]
     rows = ENVS * probes
     chips, share, stages, sub = plan(samp, cols)
@@ -46,13 +46,16 @@
     def start_of(which_core, j):
         return pl.multiple_of(which_core * (cols // 2) + j * width, 128)
 
-    def columns(which_chip):
-        return pl.ds(pl.multiple_of(which_chip * sub, 128), sub)
+    order = list(reversed(range(chips)))
 
     def load(j, away):
         at = pl.ds(start_of((1 - core) if away else core, j), width)
         return pltpu.make_async_copy(z_hbm.at[:, at], z.at[:, at], load_sem.at[j, int(away)])
 
+    small = [pltpu.make_async_copy(label_hbm, label_ref, small_sem.at[0]),
+             pltpu.make_async_copy(probes_hbm, probes_ref, small_sem.at[1])]
+    for copy in small:
+        copy.start()
     for j in range(stages):
         for away in (True, False):
             load(j, away).start()
@@ -64,6 +67,8 @@
     for peer in peers:
         pl.semaphore_signal(barrier, inc=1, device_id=peer, device_id_type=pl.DeviceIdType.MESH)
 
+    for copy in small:
+        copy.wait()
     labels = label_ref[...]
     for e in range(ENVS):
         onehot[e * probes:(e + 1) * probes, :] = jnp.broadcast_to(
@@ -94,8 +99,9 @@
             at = pl.ds(start_of((1 - core) if away else core, j), width)
             return jnp.dot(panel[...], z[:, at], preferred_element_type=jnp.float32)
 
-        def pair(j):
-            return remote(pair_out.at[op, j], pair_in.at[op, j], pair_s.at[op, j], pair_r.at[op, j],
+        def pair(j, r):
+            at = (op, j, partner(r))
+            return remote(pair_out.at[at], pair_in.at[at], pair_s.at[op, j, r], pair_r.at[op, j, r],
                           device(chip, 1 - core))
 
         def scatter(j, r):
@@ -115,16 +121,23 @@
             sent.append(copy)
 
         def away_part(j):
-            pair_out[op, j] = matmul(True, j)
+            part = matmul(True, j)
+            for k in range(chips):
+                pair_out[op, j, k] = part[:, k * sub:(k + 1) * sub]
+
+        def send_pair(j):
+            for r in order:
+                send(pair(j, r))
 
         def own_part(j):
-            mine[j] = matmul(False, j)
+            part = matmul(False, j)
+            for k in range(chips):
+                mine[j, k] = part[:, k * sub:(k + 1) * sub]
 
         def reduce_pair(j):
-            pair(j).wait_recv()
-            for r in reversed(range(1, chips)):
-                at = columns(partner(r))
-                both = mine[j, :, at] + pair_in[op, j, :, at]
+            for r in order[:-1]:
+                pair(j, r).wait_recv()
+                both = mine[j, partner(r)] + pair_in[op, j, partner(r)]
                 short = both.astype(jnp.bfloat16)
                 rest = both - short.astype(jnp.float32)
                 lost = sum_blocks(rest).astype(jnp.bfloat16)
@@ -132,8 +145,8 @@
                 send(scatter(j, r))
 
         def finish_panel(j):
-            at = columns(chip)
-            total = mine[j, :, at] + pair_in[op, j, :, at]
+            pair(j, 0).wait_recv()
+            total = mine[j, chip] + pair_in[op, j, chip]
             lost = jnp.zeros((probes, sub), jnp.float32)
             for r in range(1, chips):
                 scatter(j, r).wait_recv()
@@ -157,12 +170,12 @@
         if op == 0:
             own_part(0)
             pl.semaphore_wait(barrier, len(peers))
-        send(pair(0))
+        send_pair(0)
         if op == 1:
             own_part(0)
         for j in range(1, stages):
             away_part(j)
-            send(pair(j))
+            send_pair(j)
             reduce_pair(j - 1)
             own_part(j)
         reduce_pair(stages - 1)
@@ -217,27 +230,30 @@
         chips, _, stages, sub = plan(samp, cols)
         vmem = pltpu.VMEM
         dma = pltpu.SemaphoreType.DMA
-        out = jax.ShapeDtypeStruct((count, local), jnp.float32)
+        out = pltpu.VMEM((count, local), jnp.float32)
+        anywhere = pl.BlockSpec(memory_space=pl.ANY)
         whole = pl.BlockSpec(memory_space=pltpu.VMEM)
         return pl.pallas_call(
             functools.partial(kernel, samp, snp),
             out_shape=(out, out),
-            in_specs=[pl.BlockSpec(memory_space=pl.ANY), whole, whole, pl.BlockSpec(memory_space=pltpu.SMEM)],
+            in_specs=[anywhere, anywhere, anywhere, pl.BlockSpec(memory_space=pltpu.SMEM)],
             out_specs=(whole, whole),
             scratch_shapes=[
                 vmem((local, cols), jnp.bfloat16),
+                vmem((count, local), jnp.bfloat16),
+                vmem((1, local), jnp.int32),
                 vmem((rows, local), jnp.bfloat16),
                 vmem((rows, local), jnp.float32),
-                vmem((stages, rows, chips * sub), jnp.float32),
-                vmem((2, stages, rows, chips * sub), jnp.float32),
-                vmem((2, stages, rows, chips * sub), jnp.float32),
+                vmem((stages, chips, rows, sub), jnp.float32),
+                vmem((2, stages, chips, rows, sub), jnp.float32),
+                vmem((2, stages, chips, rows, sub), jnp.float32),
                 vmem((2, stages, chips, rows + count, sub), jnp.bfloat16),
                 vmem((2, stages, chips, rows + count, sub), jnp.bfloat16),
                 vmem((2, stages, 2, chips, rows + count, sub), jnp.bfloat16),
                 vmem((rows + count, local), jnp.float32),
                 vmem((2, snp, count, local), jnp.float32),
-                dma((stages, 2)),
-                dma((2, stages)), dma((2, stages)),
+                dma((stages, 2)), dma((2,)),
+                dma((2, stages, chips)), dma((2, stages, chips)),
                 dma((2, stages, chips)), dma((2, stages, chips)),
                 dma((2, stages, chips)), dma((2, stages, chips)),
                 dma((2, stages, chips)), dma((2, stages, chips)),

time: 46.2 us -> 45.1 us (0.976)
  local copies, waits for them, and re-layouts: 2.75 us -> 1.23 us
  Pallas kernels: 42.5 us -> 43 us
    unnamed x2, local copies, waits for them, and re-layouts: 2.75 us -> 1.23 us
    pallas_call x1, Pallas kernels: 42.5 us -> 43 us  [per_device(): pl.pallas_call(functools.partial(kernel, samp, snp), out_shape=(out, out)...]
where the time goes in v3:
time: 45.1 us; the launch traced here: 44.9 us
  Pallas kernels  43 us (95%)
  local copies, waits for them, and re-layouts  1.23 us (3%)
  between operations  0.64 us (1%)
    pallas_call x1, Pallas kernels, per_device(): pl.pallas_call(functools.partial(kernel, samp, snp), out_shape=(out, out)...  43 us
    unnamed x2, local copies, waits for them, and re-layouts  1.23 us

profile of v3, /device:TPU:0, one launch (start us, length us, event | category | flops | bytes accessed | tf_op | source)
XLA Modules:
  0.0 44.9 jit_solution(13369784418458694324)
XLA Ops:
  0.6 43.0 %shard_map.59 = (f32[8,1024]{1,0:T(8,128)S(1)}, f32[8,1024]{1,0:T(8,128)S(1)}) custom-call(bf16[1024,4096]{1,0:T(8,128)(2,1)} %z_hbm.1, bf16[8,1024]{1,0:T(8,128)(2,1)} %probes_hbm.1, s32[1,1024]{1,0:T(1,128)} %bitcast.1, f32[3]{0:T(128)} %var_ref.1), custom_call_target="tpu_custom_call" | custom-call | tf_op jit(solution)/shard_map/pallas_call | solution.py:236
  43.6 0.6 %copy.8 = f32[8,1024]{1,0:T(8,128)} copy(f32[8,1024]{1,0:T(8,128)S(1)} %get-tuple-element.2) | data formatting | bytes 65536
  44.3 0.6 %copy.9 = f32[8,1024]{1,0:T(8,128)} copy(f32[8,1024]{1,0:T(8,128)S(1)} %get-tuple-element.3) | data formatting | bytes 65536

commit v4 on v3

v4 whole, which is shorter than its diff:
```python
import functools

import jax
import jax.numpy as jnp
from jax import lax
from jax.experimental import pallas as pl
from jax.experimental.pallas import tpu as pltpu
from jax.sharding import PartitionSpec as P

ENVS = 8
OPERATOR = (0, 1, 1, 0, 1, 0, 0, 1, 1)
TURNS = (0,) + OPERATOR + (0,) + OPERATOR + (0, 1)


def plan(samp, cols):
    chips = samp // 2
    share = cols // samp
    stages = 1
    return chips, share, stages, share // stages


def kernel(
    samp, snp, z_hbm, probes_hbm, label_hbm, var_ref, first_ref, second_ref,
    z, probes_ref, label_ref, panel, onehot, state, image, mine, pair_out, pair_in, rs_out, rs_in, ag, z_in,
    load_sem, small_sem, pair_s, pair_r, rs_s, rs_r, ag_s, ag_r, fw_s, fw_r, zs_s, zs_r,
):
    probes, local = probes_hbm.shape
    cols = z.shape[1]
    rows = ENVS * probes // 2
    half = local // 2
    chips, share, stages, sub = plan(samp, cols)
    me = lax.axis_index("samp")
    chip, core = me // 2, me % 2
    here = lax.axis_index("snp")

    def device(other_chip, other_core):
        return {"samp": other_chip * 2 + other_core}

    def partner(r):
        if chips & (chips - 1):
            return lax.rem(chip + r, chips)
        return sum(lax.rem(chip // bit + r // bit, 2) * bit for bit in (1 << b for b in range(chips.bit_length() - 1)))

    def source(r):
        return lax.rem(chip - r + chips, chips) if chips & (chips - 1) else partner(r)

    width = chips * sub

    def start_of(which_core, j):
        return pl.multiple_of(which_core * (cols // 2) + j * width, 128)

    order = list(reversed(range(chips)))

    def load(j, away):
        at = pl.ds(start_of((1 - core) if away else core, j), width)
        return pltpu.make_async_copy(z_hbm.at[:, at], z.at[:, at], load_sem.at[j, int(away)])

    small = [pltpu.make_async_copy(label_hbm, label_ref, small_sem.at[0]),
             pltpu.make_async_copy(probes_hbm, probes_ref, small_sem.at[1])]
    for copy in small:
        copy.start()
    for j in range(stages):
        for away in (True, False):
            load(j, away).start()

    barrier = pltpu.get_barrier_semaphore()
    peers = [device(chip, 1 - core)]
    peers += [device(partner(r), core) for r in range(1, chips)]
    peers += [{"snp": lax.rem(here + r, snp)} for r in range(1, snp)]
    for peer in peers:
        pl.semaphore_signal(barrier, inc=1, device_id=peer, device_id_type=pl.DeviceIdType.MESH)

    for copy in small:
        copy.wait()
    labels = label_ref[...]
    upper = lax.broadcasted_iota(jnp.int32, (probes, local), 0) < probes // 2
    packed_upper = lax.broadcasted_iota(jnp.int32, (probes, half), 0) < probes // 2

    def swap(tile):
        return pltpu.roll(tile, probes // 2, 0)

    tiles = [slice(i * probes, (i + 1) * probes) for i in range(ENVS // 2)]
    for i, tile in enumerate(tiles):
        onehot[tile, :] = (jnp.broadcast_to(labels, (probes, local)) == jnp.where(upper, 2 * i, 2 * i + 1)).astype(jnp.float32)

    def remote(src, dst, send, recv, to):
        return pltpu.make_async_remote_copy(
            src_ref=src, dst_ref=dst, send_sem=send, recv_sem=recv,
            device_id=to, device_id_type=pl.DeviceIdType.MESH)

    def sum_blocks(blocks):
        total = blocks[tiles[0]]
        for tile in tiles[1:]:
            total = total + blocks[tile]
        return total + swap(total)

    sent = []

    def send(copy):
        copy.start()
        sent.append(copy)

    def chain(group):
        everything = probes_ref[...].astype(jnp.float32)
        turned = swap(everything)
        state[group] = jnp.where(upper, everything, turned) if group == 0 else jnp.where(upper, turned, everything)
        for op in range(2):
            yield from operator(group, op)

    def operator(group, op):
        first_use = group == 0 and op == 0
        loads = op == 0 and group == 0
        t = group * 2 + op
        current = state[group]
        rounded = current.astype(jnp.bfloat16).astype(jnp.float32)
        panel[group] = jnp.concatenate([onehot[tile, :] * rounded for tile in tiles], axis=0).astype(jnp.bfloat16)

        def matmul(away, j):
            if loads:
                load(j, away).wait()
            at = pl.ds(start_of((1 - core) if away else core, j), width)
            return jnp.dot(panel[group], z[:, at], preferred_element_type=jnp.float32)

        def pair(j, r):
            at = (t, j, partner(r))
            return remote(pair_out.at[at], pair_in.at[at], pair_s.at[t, j, r], pair_r.at[t, j, r],
                          device(chip, 1 - core))

        def scatter(j, r):
            return remote(rs_out.at[t, j, r], rs_in.at[t, j, r], rs_s.at[t, j, r], rs_r.at[t, j, r],
                          device(partner(r), core))

        def gather(j, r):
            at = ag.at[t, j, core, chip]
            return remote(at, at, ag_s.at[t, j, r], ag_r.at[t, j, r], device(partner(r), core))

        def forward(j, r):
            at = ag.at[t, j, core, source(r)]
            return remote(at, at, fw_s.at[t, j, r], fw_r.at[t, j, r], device(chip, 1 - core))

        def away_part(j):
            part = matmul(True, j)
            for k in range(chips):
                pair_out[t, j, k] = part[:, k * sub:(k + 1) * sub]

        def send_pair(j):
            for r in order:
                send(pair(j, r))

        def own_part(j):
            part = matmul(False, j)
            for k in range(chips):
                mine[group, k] = part[:, k * sub:(k + 1) * sub]

        def reduce_pair(j):
            for r in order[:-1]:
                pair(j, r).wait_recv()
                both = mine[group, partner(r)] + pair_in[t, j, partner(r)]
                short = both.astype(jnp.bfloat16)
                rest = both - short.astype(jnp.float32)
                lost = sum_blocks(rest).astype(jnp.bfloat16)
                rs_out[t, j, r] = jnp.concatenate([lost, short], axis=0)
                send(scatter(j, r))

        def finish_panel(j):
            pair(j, 0).wait_recv()
            total = mine[group, chip] + pair_in[t, j, chip]
            lost = jnp.zeros((probes, sub), jnp.float32)
            for r in range(1, chips):
                scatter(j, r).wait_recv()
                came = rs_in[t, j, r].astype(jnp.float32)
                total = total + came[probes:]
                lost = lost + came[:probes]
            plain = sum_blocks(total) + lost
            ag[t, j, core, chip] = jnp.concatenate([plain, total], axis=0).astype(jnp.bfloat16)
            for r in reversed(range(1, chips)):
                send(gather(j, r))
            send(forward(j, 0))

        def add_image(j, which_core, which_chip):
            at = pl.ds(pl.multiple_of(start_of(which_core, j) + which_chip * sub, 128), sub)
            part = lax.dot_general(
                ag[t, j, which_core, which_chip], z[:, at],
                (((1,), (1,)), ((), ())), preferred_element_type=jnp.float32)
            image[group] = image[group] + part

        away_part(0)
        if first_use:
            own_part(0)
            pl.semaphore_wait(barrier, len(peers))
        send_pair(0)
        if not first_use:
            own_part(0)
        yield
        reduce_pair(0)
        yield
        image[group] = jnp.zeros((rows + probes, local), jnp.float32)
        finish_panel(0)
        yield
        add_image(0, core, chip)
        for r in order[:-1]:
            gather(0, r).wait_recv()
            send(forward(0, r))
            add_image(0, core, source(r))
        yield
        for r in [0] + order[:-1]:
            forward(0, r).wait_recv()
            add_image(0, 1 - core, source(r))

        total_snps = cols * snp
        interaction = jnp.zeros((probes, local), jnp.float32)
        for i, tile in enumerate(tiles):
            interaction = interaction + onehot[tile, :] * image[group, (i + 1) * probes:(i + 2) * probes, :]
        interaction = interaction + swap(interaction)
        weighted = var_ref[0] * image[group, :probes, :] / total_snps + var_ref[1] * interaction / total_snps
        z_in[t, here] = jnp.where(packed_upper, weighted[:, :half], weighted[:, half:])

        def other_snp(r):
            return lax.rem(here + jnp.where(here < snp // 2, snp - r, r), snp)

        def over_snps(r, recv):
            return remote(z_in.at[t, here], z_in.at[t, here], zs_s.at[t, r], zs_r.at[t, recv],
                          {"snp": other_snp(r)})

        for r in range(1, snp):
            send(over_snps(r, here))
        yield
        for r in range(1, snp):
            over_snps(r, other_snp(r)).wait_recv()
        total = z_in[t, 0]
        for s in range(1, snp):
            total = total + z_in[t, s]
        turned = swap(total)
        whole = jnp.concatenate(
            [jnp.where(packed_upper, total, turned), jnp.where(packed_upper, turned, total)], axis=1)
        result = whole + var_ref[2] * state[group]
        state[group] = result
        out = first_ref if op == 0 else second_ref
        out[...] = result if group == 0 else jnp.where(upper, out[...], result)

    chains = [chain(0), chain(1)]
    for group in TURNS:
        next(chains[group], None)
    for copy in sent:
        copy.wait_send()


def solution(mesh):
    samp, snp = mesh.shape["samp"], mesh.shape["snp"]

    def per_device(genotypes, probes, env_label, variances):
        local, cols = genotypes.shape
        count = probes.shape[0]
        rows = ENVS * count // 2
        chips, _, stages, sub = plan(samp, cols)
        vmem = pltpu.VMEM
        dma = pltpu.SemaphoreType.DMA
        out = pltpu.VMEM((count, local), jnp.float32)
        anywhere = pl.BlockSpec(memory_space=pl.ANY)
        whole = pl.BlockSpec(memory_space=pltpu.VMEM)
        return pl.pallas_call(
            functools.partial(kernel, samp, snp),
            out_shape=(out, out),
            in_specs=[anywhere, anywhere, anywhere, pl.BlockSpec(memory_space=pltpu.SMEM)],
            out_specs=(whole, whole),
            scratch_shapes=[
                vmem((local, cols), jnp.bfloat16),
                vmem((count, local), jnp.bfloat16),
                vmem((1, local), jnp.int32),
                vmem((2, rows, local), jnp.bfloat16),
                vmem((rows, local), jnp.float32),
                vmem((2, count, local), jnp.float32),
                vmem((2, rows + count, local), jnp.float32),
                vmem((2, chips, rows, sub), jnp.float32),
                vmem((4, stages, chips, rows, sub), jnp.float32),
                vmem((4, stages, chips, rows, sub), jnp.float32),
                vmem((4, stages, chips, rows + count, sub), jnp.bfloat16),
                vmem((4, stages, chips, rows + count, sub), jnp.bfloat16),
                vmem((4, stages, 2, chips, rows + count, sub), jnp.bfloat16),
                vmem((4, snp, count, local // 2), jnp.float32),
                dma((stages, 2)), dma((2,)),
                dma((4, stages, chips)), dma((4, stages, chips)),
                dma((4, stages, chips)), dma((4, stages, chips)),
                dma((4, stages, chips)), dma((4, stages, chips)),
                dma((4, stages, chips)), dma((4, stages, chips)),
                dma((4, snp)), dma((4, snp)),
            ],
            compiler_params=pltpu.CompilerParams(
                collective_id=0, has_side_effects=True, vmem_limit_bytes=56 * 1024 * 1024),
        )(genotypes, probes, env_label.reshape(1, local), variances)

    return jax.shard_map(
        per_device,
        mesh=mesh,
        in_specs=(P("samp", "snp"), P(None, "samp"), P("samp"), P()),
        out_specs=(P(None, "samp"), P(None, "samp")),
        check_vma=False,
    )
```

time: 45.1 us -> 45.6 us (1.011)
  Pallas kernels: 43 us -> 43.5 us
    pallas_call x1, Pallas kernels: 43 us -> 43.5 us  [per_device(): pl.pallas_call(functools.partial(kernel, samp, snp), out_shape=(out, out)...]
where the time goes in v4:
time: 45.6 us; the launch traced here: 45.4 us
  Pallas kernels  43.5 us (95%)
  local copies, waits for them, and re-layouts  1.23 us (3%)
  between operations  0.64 us (1%)
    pallas_call x1, Pallas kernels, per_device(): pl.pallas_call(functools.partial(kernel, samp, snp), out_shape=(out, out)...  43.5 us
    unnamed x2, local copies, waits for them, and re-layouts  1.23 us

profile of v4, /device:TPU:0, one launch (start us, length us, event | category | flops | bytes accessed | tf_op | source)
XLA Modules:
  0.0 45.4 jit_solution(6578452797411067852)
XLA Ops:
  0.6 43.5 %shard_map.59 = (f32[8,1024]{1,0:T(8,128)S(1)}, f32[8,1024]{1,0:T(8,128)S(1)}) custom-call(bf16[1024,4096]{1,0:T(8,128)(2,1)} %z_hbm.1, bf16[8,1024]{1,0:T(8,128)(2,1)} %probes_hbm.1, s32[1,1024]{1,0:T(1,128)} %bitcast.1, f32[3]{0:T(128)} %var_ref.1), custom_call_target="tpu_custom_call" | custom-call | tf_op jit(solution)/shard_map/pallas_call | solution.py:261
  44.2 0.6 %copy.8 = f32[8,1024]{1,0:T(8,128)} copy(f32[8,1024]{1,0:T(8,128)S(1)} %get-tuple-element.2) | data formatting | bytes 65536
  44.8 0.6 %copy.9 = f32[8,1024]{1,0:T(8,128)} copy(f32[8,1024]{1,0:T(8,128)S(1)} %get-tuple-element.3) | data formatting | bytes 65536
